TPU v7x, 32 devices: a whole 2x2x4 slice. The times are simulated.
32 devices in a mesh: expert: 8 (over y, x, core), row: 4 (over z).
Axes of the slice: x: 2, y: 2, z: 4, core: 2. Of those that a mesh axis runs over, the one named last changes fastest.
Arguments:
- weights: bfloat16 [8, 7168, 2048], P('expert', 'row'), may hold values from -6 to 6
- left_bits: int32 [8, 7168], P('expert', 'row'), may hold values from 0 to 1
- right_bits: int32 [8, 2048], P('expert'), may hold values from 0 to 1
- groups: int32 [8, 2048], P('expert'), may hold values from 0 to 15, never falling along the last dimension, each value on 1 to 256 neighbouring positions
Outputs:
- scaled: bfloat16 [8, 7168, 2048], P('expert', 'row')
- block_error: float32 [8, 7168, 256], P('expert', 'row')
- scales: float32 [8, 16], P('expert')
- expert_error: float32 [8], P('expert')
- total_error: float32 [], replicated
Inputs may be any that keep to these rules, and one draw needn't show every extreme that they name: Along each expert's 2048 columns the group number never falls; each of the 16 groups holds 1 to 256 columns.
All inputs are finite; a program needn't handle non-finite values.
Results may differ from a plain program's by a relative error of at most 0.0091.
Values may be sent and summed in bfloat16 or wider, within the bound.
No kernel may reach another device: no remote copies, remote signals or barrier semaphores. Data moves between devices by JAX's collectives and lax.ppermute only.
A program may use at most 192 MiB of HBM per device.

v0:
```python
import math
import jax
import jax.numpy as jnp
from jax import lax
from jax.sharding import PartitionSpec as P

D = 7168
FF = 2048
HB = 128
OUTER = 16
GROUPS = 16
BLOCKS = 56


def sylvester(order):
    row_index = jnp.arange(order, dtype=jnp.int32)[:, None]
    col_index = jnp.arange(order, dtype=jnp.int32)[None, :]
    common = jnp.bitwise_and(row_index, col_index)
    parity = jnp.zeros((order, order), jnp.int32)
    for bit_pos in range(order.bit_length() - 1):
        parity = parity + jnp.bitwise_and(jnp.right_shift(common, bit_pos), 1)
    return (1 - 2 * jnp.bitwise_and(parity, 1)).astype(jnp.float32)


def cosine_block(order):
    first = jnp.arange(order, dtype=jnp.float32)[:, None]
    second = jnp.arange(order, dtype=jnp.float32)[None, :]
    table = math.sqrt(2.0 / order) * jnp.cos(math.pi * (2.0 * second + 1.0) * first / (2.0 * order))
    return jnp.where(first == 0.0, table * math.sqrt(0.5), table)


def coset_error(values):
    nearest = jnp.floor(values + 0.5)
    offset = values - nearest
    squares = jnp.sum(offset * offset, axis=-1)
    largest = jnp.max(jnp.abs(offset), axis=-1)
    parity = jnp.mod(jnp.sum(nearest, axis=-1), 2.0)
    return jnp.where(parity > 0.5, squares + 1.0 - 2.0 * largest, squares)


def lattice_error(values):
    octets = values.reshape(values.shape[:-1] + (values.shape[-1] // 8, 8))
    return jnp.minimum(coset_error(octets), coset_error(octets - 0.5))


def row_transform(mixed_rows, row_hadamard):
    turned = jnp.einsum("eibf,bk->eikf", mixed_rows, row_hadamard, precision=lax.Precision.HIGHEST)
    return turned / math.sqrt(HB)


def weight_of_rows(first_row, count):
    positions = (first_row + jnp.arange(count, dtype=jnp.int32)).astype(jnp.float32)
    return (1.0 + 4.0 * (positions + 0.5) / D) / 3.0


def group_scale(rotated, group_cols):
    column_peak = jnp.max(jnp.abs(rotated), axis=1)
    group_ids = jnp.arange(GROUPS, dtype=jnp.int32)
    in_group = group_cols[:, None, :] == group_ids[None, :, None]
    partial_peak = jnp.max(jnp.where(in_group, column_peak[:, None, :], 0.0), axis=2)
    group_peak = jnp.maximum(lax.pmax(partial_peak, "row"), 1.0)
    column_scale = jnp.sum(jnp.where(in_group, (2.0 / group_peak)[:, :, None], 0.0), axis=1)
    return (group_peak, column_scale)


def body(weights, left_bits, right_bits, groups):
    experts, local_rows, width = weights.shape
    blocks_here = local_rows // HB
    column_hadamard = sylvester(width // OUTER).astype(jnp.bfloat16)
    outer_hadamard = sylvester(OUTER)
    row_hadamard = sylvester(HB)
    block_matrix = cosine_block(BLOCKS).astype(jnp.bfloat16)
    left_sign = (2 * left_bits - 1).astype(jnp.float32)
    right_sign = (2 * right_bits - 1).astype(jnp.float32)
    signed = (weights.astype(jnp.float32) * left_sign[:, :, None] * right_sign[:, None, :]).astype(
        jnp.bfloat16
    )
    shaped = signed.reshape(experts, local_rows, OUTER, width // OUTER)
    inner = jnp.einsum("erpq,qs->erps", shaped, column_hadamard, preferred_element_type=jnp.float32)
    outer = jnp.einsum("erps,pt->erts", inner, outer_hadamard, precision=lax.Precision.HIGHEST)
    columns = (outer.reshape(experts, local_rows, width) / math.sqrt(FF)).astype(jnp.bfloat16)
    blocked = columns.reshape(experts, blocks_here, HB, width)
    own_start = lax.axis_index("row") * blocks_here
    own_matrix = lax.dynamic_slice_in_dim(block_matrix, own_start, blocks_here, 0)
    mixed_rows = jnp.einsum(
        "ij,ejbf->eibf",
        own_matrix,
        lax.all_gather(blocked, "row", axis=1, tiled=True),
        preferred_element_type=jnp.float32,
    )
    rotated = row_transform(mixed_rows, row_hadamard)
    rotated = rotated.reshape(experts, local_rows, width)
    group_peak, column_scale = group_scale(rotated, groups)
    values = rotated * column_scale[:, None, :]
    block_errors = lattice_error(values)
    row_weight = weight_of_rows(lax.axis_index("row") * local_rows, local_rows)
    partial_error = jnp.sum(block_errors * row_weight[None, :, None], axis=(1, 2)) / (D * FF // 8)
    scaled = values.astype(jnp.bfloat16)
    expert_count = experts * lax.axis_size("expert")
    expert_error = lax.psum(partial_error, "row")
    total_error = lax.psum(jnp.sum(expert_error), "expert") / expert_count
    return (scaled, block_errors, group_peak / 2.0, expert_error, total_error)


def solution(mesh):
    placed = (P("expert", "row", None), P("expert", "row"), P("expert", None), P("expert", None))
    return jax.shard_map(
        body,
        mesh=mesh,
        in_specs=placed,
        out_specs=(
            P("expert", "row", None),
            P("expert", "row", None),
            P("expert", None),
            P("expert"),
            P(),
        ),
        check_vma=False,
    )
```

profile of v0, /device:TPU:0, one launch (start us, length us, event | category | flops | bytes accessed | tf_op | source)
XLA Modules:
  0.0 734.2 jit_solution(6547402217888224501)
XLA Ops:
  7.2 0.0 all-gather.2.cloned.1.call-start
  7.2 0.7 add_convert_fusion
  7.9 0.7 convert_reduce_fusion
  8.6 5.1 fusion.8
  13.7 5.8 copy.28
  19.5 4.3 fusion.25
  23.9 15.7 %fusion.14 = bf16[1,1792,16,128]{3,2,1,0:T(8,128)(2,1)} fusion(f32[1792,16,128]{2,1,0:T(8,128)S(1)} %fusion.25), kind=kOutput, calls=%fused_computation.22 | convolution fusion | flops 711987200 | bytes 22020096 | tf_op jit(solution)/shard_map/erps,pt->erts/dot_general | solution.py:80
  39.6 11.8 %convert_element_type.76 = bf16[1,14,128,2048]{3,2,1,0:T(8,128)(2,1)} reshape(bf16[1,1792,16,128]{3,2,1,0:T(8,128)(2,1)} %fusion.14) | data formatting | bytes 14680064 | tf_op jit(solution)/shard_map/convert_element_type | solution.py:81
  51.4 0.0 all-gather.2.cloned.1.call-update
  51.4 0.1 dynamic-slice
  51.5 495.9 %all-gather.2.cloned.1.call-done = bf16[1,56,128,2048]{3,2,0,1:T(8,128)(2,1)} async-done(((bf16[1,14,128,2048]{3,2,0,1:T(8,128)(2,1)}), bf16[1,56,128,2048]{3,2,0,1:T(8,128)(2,1)}) %all-gather.2.cloned.1.call-update) | async-done | bytes 29360144 | tf_op jit(solution)/shard_map/all_gather | solution.py:88
  547.4 31.9 %fusion.9 = f32[14,128,2048]{2,0,1:T(8,128)} fusion(bf16[1,56,128,2048]{3,2,0,1:T(8,128)(2,1)} %all-gather.2.cloned.1.call-done, s32[]{:T(128)S(6)} %select_n.94, f32[56]{0:T(128)S(1)} %add_multiply_fusion.2, pred[14]{0:T(512)(128)(4,1)S(1)} %dynamic-slice), kind=kOutput, calls=%fused_computation.21 | convolution fusion | flops 411048064 | bytes 44040432 | tf_op jit(solution)/shard_map/ij,ejbf->eibf/dot_general | solution.py:85
  579.3 0.0 copy-start
  579.3 29.6 %abs_reduce_fusion.2 = (f32[2048]{0:T(1024)S(1)}, f32[128,14,2048]{2,0,1:T(8,128)}) fusion(f32[14,128,2048]{2,0,1:T(8,128)} %fusion.9), kind=kOutput, calls=%fused_computation.15 | convolution fusion | flops 5648562176 | bytes 29368320 | tf_op jit(solution)/shard_map/eibf,bk->eikf/dot_general | solution.py:47
  608.9 0.0 copy-done
  608.9 0.1 select_reduce_fusion.1
  609.0 8.9 %pmax.7 = f32[1,16]{1,0:T(1,128)S(1)} all-reduce(f32[1,16]{1,0:T(1,128)S(1)} %bitcast.114), channel_id=1, replica_groups=mesh['expert'=8,'row'=4] {'row'}, use_global_device_ids=true, to_apply=%region_2.3 | all-reduce | flops 16 | bytes 128 | tf_op jit(solution)/shard_map/pmax | solution.py:61
  617.9 0.5 maximum_multiply_fusion
  618.4 0.1 select_reduce_fusion
  618.5 0.1 mul.276
  618.6 10.4 %fusion.3 = bf16[1,1792,2048]{2,1,0:T(8,128)(2,1)} fusion(f32[128,14,2048]{2,0,1:T(8,128)} %get-tuple-element.26, f32[2048]{0:T(1024)S(1)} %select_reduce_fusion), kind=kLoop, calls=%fused_computation.4 | loop fusion | flops 7340032 | bytes 22028288 | tf_op jit(solution)/shard_map/convert_element_type | solution.py:98
  629.0 17.6 %copy.24 = f32[1,14,128,2048]{2,1,3,0:T(8,128)} copy(f32[1,14,128,2048]{3,2,1,0:T(8,128)} %bitcast.108) | data formatting | bytes 29360128 | tf_op jit(solution)/shard_map/div | solution.py:48
  646.6 16.9 %reshape.599 = f32[1,1792,256,8]{1,3,2,0:T(8,128)} reshape(f32[1,14,128,2048]{2,1,3,0:T(8,128)} %copy.24) | data formatting | bytes 29360128 | tf_op jit(solution)/shard_map/reshape | solution.py:92
  663.5 32.5 %fusion.7 = (f32[1792,256]{0,1:T(8,128)S(1)}, f32[1792,256]{0,1:T(8,128)S(1)}, f32[1792,256]{0,1:T(8,128)S(1)}, f32[1792,256]{0,1:T(8,128)S(1)}, f32[1792,256]{0,1:T(8,128)S(1)}, /*index=5*/f32[1792,256]{0,1:T(8,128)S(1)}) fusion(f32[1,1792,256,8]{1,3,2,0:T(8,128)} %reshape.599, f32[256,8]{1,0:T(8,128)S(1)} %mul.276), kind=kLoop, calls=%fused_computation.14 | loop fusion | flops 59637760 | bytes 25698304 | tf_op jit(solution)/shard_map/reduce_sum | solution.py:37
  696.0 3.2 multiply_reduce_fusion.2
  699.3 1.7 copy.25
  701.6 11.3 %psum.14 = f32[1]{0:T(128)} all-reduce(f32[1]{0:T(128)} %bitcast.25), channel_id=1, replica_groups=mesh['expert'=8,'row'=4] {'row'}, use_global_device_ids=true, to_apply=%region_11.12 | all-reduce | flops 1 | bytes 8 | tf_op jit(solution)/shard_map/psum | solution.py:100
  712.9 12.4 %psum.15 = f32[]{:T(128)} all-reduce(f32[]{:T(128)} %bitcast.26), channel_id=1, replica_groups=mesh['expert'=8,'row'=4] {'expert'}, use_global_device_ids=true, to_apply=%region_12.13 | all-reduce | flops 1 | bytes 8 | tf_op jit(solution)/shard_map/psum | solution.py:101
  (3 shorter events, 0.0 us)
Async XLA Ops:
  7.2 540.2 %all-gather.2.cloned.1.call-start = ((), (), s32[]{:S(2)}) async-start(), calls=%async_computation | async-start | bytes 36700160 | tf_op jit(solution)/shard_map/all_gather | solution.py:88
  579.3 29.6 %copy-start = (s32[1,2048]{1,0:T(1,128)S(1)}, s32[1,2048]{1,0:T(1,128)}, u32[]{:S(2)}) copy-start(s32[1,2048]{1,0:T(1,128)} %param.7) | copy-start | bytes 24580
Sparse Core Ops, SparseCore 0:
  51.5 495.8 all-gather.1
where the time goes:
time: 743 us; the launch traced here: 734 us
  waiting for transfers between devices  496 us (67%)
  matrix products  81.6 us (11%)
  local copies, waits for them, and re-layouts  53.9 us (7%)
  other arithmetic  53.5 us (7%)
  blocking collectives  32.6 us (4%)
  between operations  16.7 us (2%)
    all_gather x1, waiting for transfers between devices, body(): lax.all_gather(blocked, 'row', axis=1, tiled=True)  496 us
    reduce_sum x1, other arithmetic, coset_error(): parity = jnp.mod(jnp.sum(nearest, axis=-1), 2.0)  32.5 us
    dot_general x1, matrix products, body(): jnp.einsum('ij,ejbf->eibf', own_matrix, lax.all_gather(blocked, 'row', ax...  31.9 us
    dot_general x1, matrix products, row_transform(): jnp.einsum('eibf,bk->eikf', mixed_rows, row_hadamard, precision=lax.Preci...  29.6 us
    div x1, local copies, waits for them, and re-layouts, row_transform(): return turned / math.sqrt(HB)  17.6 us
    reshape x1, local copies, waits for them, and re-layouts, body(): rotated = rotated.reshape(experts, local_rows, width)  16.9 us
    dot_general x1, matrix products, body(): jnp.einsum('erps,pt->erts', inner, outer_hadamard, precision=lax.Precisio...  15.7 us
  transfers between devices with their start and end apart: 1, of which 1 were waited for; matrix products, arithmetic and copies ran while one was open for 0% of the time, Pallas kernels for 0%

commit v1 on v0

--- a/solution.py
+++ b/solution.py
@@ -82,12 +82,38 @@
     blocked = columns.reshape(experts, blocks_here, HB, width)
     own_start = lax.axis_index("row") * blocks_here
     own_matrix = lax.dynamic_slice_in_dim(block_matrix, own_start, blocks_here, 0)
-    mixed_rows = jnp.einsum(
+    size, position, span = (lax.axis_size("row"), lax.axis_index("row"), blocked.shape[1])
+    ahead = [(i, (i + 1) % size) for i in range(size)]
+    downward = [(i, (i - 1) % size) for i in range(size)]
+    middle = size // 2
+    from_left = from_right = blocked
+    running = jnp.einsum(
         "ij,ejbf->eibf",
-        own_matrix,
-        lax.all_gather(blocked, "row", axis=1, tiled=True),
+        lax.dynamic_slice_in_dim(own_matrix, position * span, blocked.shape[1], axis=1),
+        blocked,
         preferred_element_type=jnp.float32,
     )
+    for lap in range(1, middle + 1):
+        from_left = lax.ppermute(from_left, "row", ahead)
+        if lap < size - middle:
+            from_right = lax.ppermute(from_right, "row", downward)
+            running = running + jnp.einsum(
+                "ij,ejbf->eibf",
+                lax.dynamic_slice_in_dim(
+                    own_matrix, (position + lap) % size * span, from_right.shape[1], axis=1
+                ),
+                from_right,
+                preferred_element_type=jnp.float32,
+            )
+        running = running + jnp.einsum(
+            "ij,ejbf->eibf",
+            lax.dynamic_slice_in_dim(
+                own_matrix, (position - lap) % size * span, from_left.shape[1], axis=1
+            ),
+            from_left,
+            preferred_element_type=jnp.float32,
+        )
+    mixed_rows = running
     rotated = row_transform(mixed_rows, row_hadamard)
     rotated = rotated.reshape(experts, local_rows, width)
     group_peak, column_scale = group_scale(rotated, groups)

time: 743 us -> 712 us (0.958)
  waiting for transfers between devices: 496 us -> 421 us
  matrix products: 81.6 us -> 122 us
  between operations: 16.7 us -> 3.38 us
  local copies, waits for them, and re-layouts: 53.9 us -> 65.9 us
    all_gather x1 -> x0, waiting for transfers between devices: 496 us -> none  [body(): lax.all_gather(blocked, 'row', axis=1, tiled=True)]
    ppermute x0 -> x3, waiting for transfers between devices: none -> 421 us  [the longest x2 303 us: body(): from_left = lax.ppermute(from_left, 'row', ahead)]
    dot_general x1 -> x4, matrix products: 31.9 us -> 72 us  [the longest x3 58.7 us: body(): jnp.einsum('ij,ejbf->eibf', lax.dynamic_slice_in_dim(own_matrix, (positio...]
    convert_element_type x1 -> x2, local copies, waits for them, and re-layouts: 11.8 us -> 23.8 us  [body(): (outer.reshape(experts, local_rows, width) / math.sqrt(FF)).astype(jnp.bf...]
  transfers between devices with their start and end apart: 1 -> 3, of which waited for: 1 -> 3; matrix products, arithmetic and copies ran while one was open for 0% -> 7% of each run, Pallas kernels for 0% -> 0%
where the time goes in v1:
time: 712 us; the launch traced here: 703 us
  waiting for transfers between devices  421 us (59%)
  matrix products  122 us (17%)
  local copies, waits for them, and re-layouts  65.9 us (9%)
  other arithmetic  53.6 us (8%)
  blocking collectives  32.5 us (5%)
    ppermute x2, waiting for transfers between devices, body(): from_left = lax.ppermute(from_left, 'row', ahead)  303 us
    ppermute x1, waiting for transfers between devices, body(): from_right = lax.ppermute(from_right, 'row', downward)  117 us
    dot_general x3, matrix products, body(): jnp.einsum('ij,ejbf->eibf', lax.dynamic_slice_in_dim(own_matrix, (positio...  58.7 us
    reduce_sum x1, other arithmetic, coset_error(): parity = jnp.mod(jnp.sum(nearest, axis=-1), 2.0)  32.5 us
    dot_general x1, matrix products, row_transform(): jnp.einsum('eibf,bk->eikf', mixed_rows, row_hadamard, precision=lax.Preci...  29.8 us
    convert_element_type x2, local copies, waits for them, and re-layouts, body(): (outer.reshape(experts, local_rows, width) / math.sqrt(FF)).astype(jnp.bf...  23.8 us
    div x1, local copies, waits for them, and re-layouts, row_transform(): return turned / math.sqrt(HB)  17.6 us
    reshape x1, local copies, waits for them, and re-layouts, body(): rotated = rotated.reshape(experts, local_rows, width)  16.9 us
  transfers between devices with their start and end apart: 3, of which 3 were waited for; matrix products, arithmetic and copies ran while one was open for 7% of the time, Pallas kernels for 0%

profile of v1, /device:TPU:0, one launch (start us, length us, event | category | flops | bytes accessed | tf_op | source)
XLA Modules:
  0.0 702.9 jit_solution(1040418867652502322)
XLA Ops:
  0.6 0.7 add_convert_fusion
  1.3 0.7 convert_reduce_fusion
  2.1 5.1 fusion.16
  7.1 5.8 copy.36
  12.9 4.3 fusion.32
  17.3 15.7 %fusion.21 = bf16[1,1792,16,128]{3,2,1,0:T(8,128)(2,1)} fusion(f32[1792,16,128]{2,1,0:T(8,128)S(1)} %fusion.32), kind=kOutput, calls=%fused_computation.30 | convolution fusion | flops 711987200 | bytes 22020096 | tf_op jit(solution)/shard_map/erps,pt->erts/dot_general | solution.py:80
  33.0 11.8 %convert_element_type.90 = bf16[1,14,128,2048]{3,2,1,0:T(8,128)(2,1)} reshape(bf16[1,1792,16,128]{3,2,1,0:T(8,128)(2,1)} %fusion.21) | data formatting | bytes 14680064 | tf_op jit(solution)/shard_map/convert_element_type | solution.py:81
  44.8 3.1 collective-permute-start.1
  47.9 2.0 collective-permute-start
  49.9 159.2 %collective-permute-done.1 = bf16[1,14,128,2048]{3,2,1,0:T(8,128)(2,1)} collective-permute-done((bf16[1,14,128,2048]{3,2,1,0:T(8,128)(2,1)}, bf16[1,14,128,2048]{3,2,1,0:T(8,128)(2,1)}, u32[]{:S(2)}, u32[]{:S(2)}) %collective-permute-start.1) | collective-permute-done | bytes 7340064 | tf_op jit(solution)/shard_map/ppermute | solution.py:97
  209.1 0.0 collective-permute-start.2
  209.1 12.0 %convert_element_type.88 = bf16[14,128,2048]{2,1,0:T(8,128)(2,1)} reshape(bf16[1,1792,16,128]{3,2,1,0:T(8,128)(2,1)} %fusion.21) | data formatting | bytes 14680064 | tf_op jit(solution)/shard_map/convert_element_type | solution.py:81
  221.2 0.1 select_convert_fusion
  221.3 13.3 %fusion.14 = f32[128,2048,14]{1,2,0:T(8,128)} fusion(bf16[14,128,2048]{2,1,0:T(8,128)(2,1)} %convert_element_type.88, bf16[56,56]{1,0:T(8,128)(2,1)S(1)} %select_convert_fusion, s32[]{:T(128)S(6)} %select_n.134), kind=kOutput, calls=%fused_computation.26 | convolution fusion | flops 102760448 | bytes 22024196 | tf_op jit(solution)/shard_map/ij,ejbf->eibf/dot_general | solution.py:90
  234.6 13.3 %fusion.7 = f32[128,2048,14]{1,2,0:T(8,128)} fusion(bf16[1,14,128,2048]{3,2,1,0:T(8,128)(2,1)} %collective-permute-done.1, bf16[56,56]{1,0:T(8,128)(2,1)S(1)} %select_convert_fusion, s32[]{:T(128)S(6)} %select_n.134, s32[]{:T(128)S(6)} %select_n.140), kind=kOutput, calls=%fused_computation.19 | convolution fusion | flops 102760448 | bytes 22024200 | tf_op jit(solution)/shard_map/ij,ejbf->eibf/dot_general | solution.py:108
  248.0 117.2 %collective-permute-done = bf16[1,14,128,2048]{3,2,1,0:T(8,128)(2,1)} collective-permute-done((bf16[1,14,128,2048]{3,2,1,0:T(8,128)(2,1)}, bf16[1,14,128,2048]{3,2,1,0:T(8,128)(2,1)}, u32[]{:S(2)}, u32[]{:S(2)}) %collective-permute-start) | collective-permute-done | bytes 7340064 | tf_op jit(solution)/shard_map/ppermute | solution.py:99
  365.2 13.5 %fusion.9 = f32[128,2048,14]{1,2,0:T(8,128)} fusion(bf16[1,14,128,2048]{3,2,1,0:T(8,128)(2,1)} %collective-permute-done, bf16[56,56]{1,0:T(8,128)(2,1)S(1)} %select_convert_fusion, s32[]{:T(128)S(6)} %select_n.134, s32[]{:T(128)S(6)} %select_n.137), kind=kOutput, calls=%fused_computation.21 | convolution fusion | flops 102760448 | bytes 22024200 | tf_op jit(solution)/shard_map/ij,ejbf->eibf/dot_general | solution.py:100
  378.7 144.1 %collective-permute-done.2 = bf16[1,14,128,2048]{3,2,1,0:T(8,128)(2,1)} collective-permute-done((bf16[1,14,128,2048]{3,2,1,0:T(8,128)(2,1)}, bf16[1,14,128,2048]{3,2,1,0:T(8,128)(2,1)}, u32[]{:S(2)}, u32[]{:S(2)}) %collective-permute-start.2) | collective-permute-done | bytes 7340064 | tf_op jit(solution)/shard_map/ppermute | solution.py:97
  522.8 31.9 %add_bitcast_fusion = f32[14,128,2048]{2,0,1:T(8,128)} fusion(f32[128,2048,14]{1,2,0:T(8,128)} %fusion.7, f32[128,2048,14]{1,2,0:T(8,128)} %fusion.14, f32[128,2048,14]{1,2,0:T(8,128)} %fusion.9, bf16[1,14,128,2048]{3,2,1,0:T(8,128)(2,1)} %collective-permute-done.2, bf16[56,56]{1,0:T(8,128)(2,1)S(1)} %select_convert_fusion, s32[]{:T(128)S(6)} %select_n.134, ...), kind=kOutput, calls=%fused_computation | convolution fusion | flops 113770496 | bytes 66064392 | tf_op jit(solution)/shard_map/ij,ejbf->eibf/dot_general | solution.py:108
  554.7 0.0 copy-start
  554.7 29.8 %abs_reduce_fusion.2 = (f32[2048]{0:T(1024)S(1)}, f32[128,14,2048]{2,0,1:T(8,128)}) fusion(f32[14,128,2048]{2,0,1:T(8,128)} %add_bitcast_fusion), kind=kOutput, calls=%fused_computation.13 | convolution fusion | flops 5648562176 | bytes 29368320 | tf_op jit(solution)/shard_map/eibf,bk->eikf/dot_general | solution.py:47
  584.5 0.0 copy-done
  584.5 0.1 select_reduce_fusion.1
  584.7 10.2 %pmax.7 = f32[1,16]{1,0:T(1,128)S(1)} all-reduce(f32[1,16]{1,0:T(1,128)S(1)} %bitcast.129), channel_id=1, replica_groups=mesh['expert'=8,'row'=4] {'row'}, use_global_device_ids=true, to_apply=%region_2.3 | all-reduce | flops 16 | bytes 128 | tf_op jit(solution)/shard_map/pmax | solution.py:61
  594.9 0.5 maximum_multiply_fusion
  595.4 0.1 select_reduce_fusion
  595.5 0.1 mul.331
  595.6 10.4 %fusion = bf16[1,1792,2048]{2,1,0:T(8,128)(2,1)} fusion(f32[128,14,2048]{2,0,1:T(8,128)} %get-tuple-element.26, f32[2048]{0:T(1024)S(1)} %select_reduce_fusion), kind=kLoop, calls=%fused_computation.2 | loop fusion | flops 7340032 | bytes 22028288 | tf_op jit(solution)/shard_map/convert_element_type | solution.py:124
  606.0 17.6 %copy.32 = f32[1,14,128,2048]{2,1,3,0:T(8,128)} copy(f32[1,14,128,2048]{3,2,1,0:T(8,128)} %bitcast.124) | data formatting | bytes 29360128 | tf_op jit(solution)/shard_map/div | solution.py:48
  623.6 16.9 %reshape.621 = f32[1,1792,256,8]{1,3,2,0:T(8,128)} reshape(f32[1,14,128,2048]{2,1,3,0:T(8,128)} %copy.32) | data formatting | bytes 29360128 | tf_op jit(solution)/shard_map/reshape | solution.py:118
  640.5 32.5 %fusion.4 = (f32[1792,256]{0,1:T(8,128)S(1)}, f32[1792,256]{0,1:T(8,128)S(1)}, f32[1792,256]{0,1:T(8,128)S(1)}, f32[1792,256]{0,1:T(8,128)S(1)}, f32[1792,256]{0,1:T(8,128)S(1)}, /*index=5*/f32[1792,256]{0,1:T(8,128)S(1)}) fusion(f32[1,1792,256,8]{1,3,2,0:T(8,128)} %reshape.621, f32[256,8]{1,0:T(8,128)S(1)} %mul.331), kind=kLoop, calls=%fused_computation.12 | loop fusion | flops 59637760 | bytes 25698304 | tf_op jit(solution)/shard_map/reduce_sum | solution.py:37
  673.0 3.2 multiply_reduce_fusion.2
  676.3 1.7 copy.33
  678.6 9.9 %psum.14 = f32[1]{0:T(128)} all-reduce(f32[1]{0:T(128)} %bitcast.30), channel_id=1, replica_groups=mesh['expert'=8,'row'=4] {'row'}, use_global_device_ids=true, to_apply=%region_11.12 | all-reduce | flops 1 | bytes 8 | tf_op jit(solution)/shard_map/psum | solution.py:126
  688.5 12.4 %psum.15 = f32[]{:T(128)} all-reduce(f32[]{:T(128)} %bitcast.31), channel_id=1, replica_groups=mesh['expert'=8,'row'=4] {'expert'}, use_global_device_ids=true, to_apply=%region_12.13 | all-reduce | flops 1 | bytes 8 | tf_op jit(solution)/shard_map/psum | solution.py:127
  (3 shorter events, 0.0 us)
Async XLA Ops:
  44.8 164.3 %collective-permute-start.1 = (bf16[1,14,128,2048]{3,2,1,0:T(8,128)(2,1)}, bf16[1,14,128,2048]{3,2,1,0:T(8,128)(2,1)}, u32[]{:S(2)}, u32[]{:S(2)}) collective-permute-start(bf16[1,14,128,2048]{3,2,1,0:T(8,128)(2,1)} %convert_element_type.90), channel_id=1, source_target_pairs={{0,1},{1,2},{2,3},{3,0},{4,5},{5,6},{6,7},{7,4},{8,9},{9,10},{10,1... | collective-permute-start | bytes 22020104 | tf_op jit(solution)/shard_map/ppermute | solution.py:97
  47.9 317.3 %collective-permute-start = (bf16[1,14,128,2048]{3,2,1,0:T(8,128)(2,1)}, bf16[1,14,128,2048]{3,2,1,0:T(8,128)(2,1)}, u32[]{:S(2)}, u32[]{:S(2)}) collective-permute-start(bf16[1,14,128,2048]{3,2,1,0:T(8,128)(2,1)} %convert_element_type.90), channel_id=1, source_target_pairs={{0,3},{1,0},{2,1},{3,2},{4,7},{5,4},{6,5},{7,6},{8,11},{9,8},{10,9... | collective-permute-start | bytes 22020104 | tf_op jit(solution)/shard_map/ppermute | solution.py:99
  209.1 313.7 %collective-permute-start.2 = (bf16[1,14,128,2048]{3,2,1,0:T(8,128)(2,1)}, bf16[1,14,128,2048]{3,2,1,0:T(8,128)(2,1)}, u32[]{:S(2)}, u32[]{:S(2)}) collective-permute-start(bf16[1,14,128,2048]{3,2,1,0:T(8,128)(2,1)} %collective-permute-done.1), channel_id=1, source_target_pairs={{0,1},{1,2},{2,3},{3,0},{4,5},{5,6},{6,7},{7,4},{8,9},{9,10},{10,1... | collective-permute-start | bytes 22020104 | tf_op jit(solution)/shard_map/ppermute | solution.py:97
  554.7 29.8 %copy-start = (s32[1,2048]{1,0:T(1,128)S(1)}, s32[1,2048]{1,0:T(1,128)}, u32[]{:S(2)}) copy-start(s32[1,2048]{1,0:T(1,128)} %param.7) | copy-start | bytes 24580
